TPU v7x, 32 devices: a whole 2x2x4 slice. The times are simulated.
32 devices in a mesh: dp: 8 (over y, x, core), expert: 4 (over z).
Axes of the slice: x: 2, y: 2, z: 4, core: 2. Of those that a mesh axis runs over, the one named last changes fastest.
Arguments:
- tokens: bfloat16 [4096, 2048], P(('dp', 'expert')), may hold values from -6 to 6
- cotangent: bfloat16 [4096, 2048], P(('dp', 'expert')), may hold values from -6 to 6
- expert_ids: int32 [4096, 2], P(('dp', 'expert')), may hold values from 0 to 3, all different within a row; in each aligned block of 128 rows (0 to 127, 128 to 255, ...) at most 128 rows name the same one
- combine: float32 [4096, 2], P(('dp', 'expert')), may hold values from 0.1 to 1
- w_gate: bfloat16 [4, 2048, 768], P('expert'), may hold values from -0.125 to 0.125
- w_up: bfloat16 [4, 2048, 768], P('expert'), may hold values from -0.125 to 0.125
- w_down: bfloat16 [4, 768, 2048], P('expert'), may hold values from -0.21875 to 0.21875
Outputs:
- input_grad: bfloat16 [4096, 2048], P(('dp', 'expert'))
- combine_grad: float32 [4096, 2], P(('dp', 'expert'))
- gate_grad: bfloat16 [4, 2048, 768], P('expert', 'dp')
- up_grad: bfloat16 [4, 2048, 768], P('expert', 'dp')
- down_grad: bfloat16 [4, 768, 2048], P('expert', 'dp')
Inputs may be any that keep to these rules, and one draw needn't show every extreme that they name: `expert_ids`: each token names 2 different experts. In the rows of one device no expert is named by more than 128 tokens, and in some devices' rows some expert is named by exactly 128.
All inputs are finite; a program needn't handle non-finite values.
Results may differ from a plain program's by a relative error of at most 0.02.
Values may be sent and summed in bfloat16 or wider, within the bound.
A program may use at most 128 MiB of HBM per device.

v0:
```python
import jax
import jax.numpy as jnp
from jax import lax
from jax.sharding import PartitionSpec as P


def slot_table(expert_ids, experts_all, capacity):
    pairs = expert_ids.reshape(-1)
    count = pairs.shape[0]
    onehot = (pairs[:, None] == jnp.arange(experts_all, dtype=jnp.int32)[None, :]).astype(jnp.int32)
    before = jnp.cumsum(onehot, axis=0) - onehot
    position = jnp.sum(before * onehot, axis=1)
    dest = pairs * capacity + position
    filled = (
        jnp.zeros((experts_all * capacity,), jnp.int32)
        .at[dest]
        .set(jnp.arange(count, dtype=jnp.int32) + 1)
    )
    return (dest, filled)


def gather_rows(tokens, cotangent, combine, filled, top):
    live = filled > 0
    pair = jnp.maximum(filled - 1, 0)
    source = pair // top
    rows_x = jnp.where(live[:, None], jnp.take(tokens, source, axis=0), jnp.zeros((), tokens.dtype))
    rows_dy = jnp.where(
        live[:, None], jnp.take(cotangent, source, axis=0), jnp.zeros((), cotangent.dtype)
    )
    rows_c = jnp.where(
        live, jnp.take(combine.reshape(-1), pair, axis=0), jnp.zeros((), combine.dtype)
    )
    return (rows_x, rows_dy, rows_c)


def forward_part(rows_x, gate_mat, up_mat, down_mat):
    gate = jnp.dot(rows_x, gate_mat, preferred_element_type=jnp.float32)
    up = jnp.dot(rows_x, up_mat, preferred_element_type=jnp.float32)
    sig = jax.nn.sigmoid(gate)
    act = gate * sig
    hidden = (act * up).astype(jnp.bfloat16)
    output = jnp.dot(hidden, down_mat, preferred_element_type=jnp.float32)
    return (gate, up, sig, act, hidden, output)


def backward_part(state, rows_dy, rows_c, gate_mat, up_mat, down_mat):
    gate, up, sig, act, hidden, output = state
    comb_grad = jnp.sum(rows_dy.astype(jnp.float32) * output, axis=1)
    scaled = (rows_c[:, None] * rows_dy.astype(jnp.float32)).astype(jnp.bfloat16)
    last = (((1,), (1,)), ((), ()))
    hidden_grad = lax.dot_general(scaled, down_mat, last, preferred_element_type=jnp.float32)
    gate_d = (hidden_grad * up * (sig * (1.0 + gate * (1.0 - sig)))).astype(jnp.bfloat16)
    up_d = (hidden_grad * act).astype(jnp.bfloat16)
    row_grad = lax.dot_general(gate_d, gate_mat, last, preferred_element_type=jnp.float32)
    row_grad = (
        row_grad + lax.dot_general(up_d, up_mat, last, preferred_element_type=jnp.float32)
    ).astype(jnp.bfloat16)
    return (comb_grad, scaled, gate_d, up_d, row_grad)


def shards(tokens, cotangent, expert_ids, combine, w_gate, w_up, w_down):
    first = (((0,), (0,)), ((), ()))
    local_experts = w_gate.shape[0]
    groups = lax.axis_size("expert")
    replicas = lax.axis_size("dp")
    experts_all = local_experts * groups
    tok_rows, top = expert_ids.shape
    feature = tokens.shape[1]
    hidden_width = w_gate.shape[2]
    capacity = 2 * tok_rows * top // experts_all
    dest, filled = slot_table(expert_ids, experts_all, capacity)
    rows_x, rows_dy, rows_c = gather_rows(tokens, cotangent, combine, filled, top)
    rows_x = rows_x.reshape(experts_all, capacity, feature)
    rows_dy = rows_dy.reshape(experts_all, capacity, feature)
    rows_c = rows_c.reshape(experts_all, capacity)
    recv_x, recv_dy, recv_c = (
        lax.all_to_all(rows_x, "expert", split_axis=0, concat_axis=1, tiled=True),
        lax.all_to_all(rows_dy, "expert", split_axis=0, concat_axis=1, tiled=True),
        lax.all_to_all(
            rows_c.astype(jnp.bfloat16), "expert", split_axis=0, concat_axis=1, tiled=True
        ).astype(rows_c.dtype),
    )
    states = forward_part(recv_x[0], w_gate[0], w_up[0], w_down[0])
    comb_grad, scaled, gate_d, up_d, row_grad = backward_part(
        states, recv_dy[0], recv_c[0], w_gate[0], w_up[0], w_down[0]
    )
    row_list = [row_grad]
    comb_list = [comb_grad]
    inputs = recv_x[0]
    hidden = states[4]
    paired = jnp.concatenate([gate_d, up_d], axis=1)

    def gate_up_term(start, count, inputs=inputs, paired=paired):
        return lax.dot_general(inputs, paired, first, preferred_element_type=jnp.float32)

    def down_term(start, count, hidden=hidden, scaled=scaled):
        return lax.dot_general(hidden, scaled, first, preferred_element_type=jnp.float32)

    both = lax.psum_scatter(
        gate_up_term(jnp.int32(0), feature // replicas * lax.axis_size("dp")).astype(jnp.bfloat16),
        "dp",
        scatter_dimension=0,
        tiled=True,
    ).astype(jnp.float32)
    gate_terms = [both[:, :hidden_width].astype(jnp.bfloat16)]
    up_terms = [both[:, hidden_width:].astype(jnp.bfloat16)]
    down_sum = lax.psum_scatter(
        down_term(jnp.int32(0), hidden_width // replicas * lax.axis_size("dp")).astype(
            jnp.bfloat16
        ),
        "dp",
        scatter_dimension=0,
        tiled=True,
    )
    down_terms = [down_sum]
    gate_grad = jnp.stack(gate_terms)
    up_grad = jnp.stack(up_terms)
    down_grad = jnp.stack(down_terms)
    back_rows, back_comb = (
        lax.all_to_all(jnp.stack(row_list), "expert", split_axis=1, concat_axis=0, tiled=True),
        lax.all_to_all(
            jnp.stack(comb_list).astype(jnp.bfloat16),
            "expert",
            split_axis=1,
            concat_axis=0,
            tiled=True,
        ).astype(jnp.float32),
    )
    flat_rows = back_rows.reshape(experts_all * capacity, feature)
    picked = jnp.take(flat_rows, dest, axis=0).reshape(tok_rows, top, feature)
    input_grad = jnp.sum(picked.astype(jnp.float32), axis=1).astype(jnp.bfloat16)
    combine_grad = jnp.take(back_comb.reshape(-1), dest, axis=0).reshape(tok_rows, top)
    return (input_grad, combine_grad, gate_grad, up_grad, down_grad)


def solution(mesh):
    placed = (
        P(("dp", "expert"), None),
        P(("dp", "expert"), None),
        P(("dp", "expert"), None),
        P(("dp", "expert"), None),
        P("expert", None, None),
        P("expert", None, None),
        P("expert", None, None),
    )
    return jax.shard_map(
        shards,
        mesh=mesh,
        in_specs=placed,
        out_specs=(
            P(("dp", "expert"), None),
            P(("dp", "expert"), None),
            P("expert", "dp", None),
            P("expert", "dp", None),
            P("expert", "dp", None),
        ),
        check_vma=False,
    )
```

profile of v0, /device:TPU:0, one launch (start us, length us, event | category | flops | bytes accessed | tf_op | source)
XLA Modules:
  0.0 287.7 jit_solution(16933779392859275133)
XLA Ops:
  12.6 3.4 %gather_fusion = bf16[512]{0:T(512)(128)(2,1)S(1)} fusion(bf16[256]{0:T(256)(128)(2,1)S(1)} %reshape.180, s32[1024]{0:T(1024)S(1)} %pad_clamp_fusion.2), kind=kCustom, calls=%fused_computation.2 | custom fusion | bytes 4096 | tf_op jit(solution)/shard_map/jit(_take)/gather | solution.py:31
  16.6 6.3 %all-to-all-start = ((bf16[4,1,128]{2,1,0:T(2,128)(2,1)}), bf16[4,1,128]{2,1,0:T(2,128)(2,1)S(1)}, u32[]{:S(2)}, u32[]{:S(2)}) async-start(bf16[4,1,128]{2,1,0:T(2,128)(2,1)} %copy.36), calls=%async_computation | async-start | bytes 4096 | tf_op jit(solution)/shard_map/all_to_all | solution.py:79
  23.0 6.3 %gather_fusion.4 = bf16[512,2048]{1,0:T(8,128)(2,1)} fusion(bf16[128,2048]{1,0:T(8,128)(2,1)} %param.9, s32[1024]{0:T(1024)S(1)} %pad_clamp_fusion.1), kind=kCustom, calls=%fused_computation.1.clone | custom fusion | bytes 4196352 | tf_op jit(solution)/shard_map/jit(_take)/gather | solution.py:26
  29.3 6.4 %gather_fusion.3 = bf16[512,2048]{1,0:T(8,128)(2,1)} fusion(bf16[128,2048]{1,0:T(8,128)(2,1)} %param.10, s32[1024]{0:T(1024)S(1)} %pad_clamp_fusion.1), kind=kCustom, calls=%fused_computation.clone | custom fusion | bytes 4196352 | tf_op jit(solution)/shard_map/jit(_take)/gather | solution.py:28
  35.7 4.0 %select_select_fusion.1 = (bf16[512,2048]{1,0:T(8,128)(2,1)}, bf16[512,2048]{1,0:T(8,128)(2,1)}) fusion(bf16[512,2048]{1,0:T(8,128)(2,1)} %gather_fusion.3, pred[512]{0:T(512)(128)(4,1)S(1)} %get-tuple-element.25, pred[512]{0:T(512)(128)(4,1)S(1)} %get-tuple-element.24, bf16[512,2048]{1,0:T(8,128)(2,1)} %gather_fusion.4), kind=kLoop, calls=%fused_computation.29 | loop fusion | flops 4194304 | bytes 8389632 | tf_op jit(solution)/shard_map/jit(_where)/select_n | solution.py:27
  39.7 52.8 %all_to_all.22 = bf16[4,128,2048]{2,1,0:T(8,128)(2,1)} all-to-all(bf16[4,128,2048]{2,1,0:T(8,128)(2,1)} %bitcast.90), channel_id=1, replica_groups=mesh['dp'=8,'expert'=4] {'expert'}, dimensions={0} | all-to-all | bytes 4194304 | tf_op jit(solution)/shard_map/all_to_all | solution.py:77
  92.5 4.5 %all-to-all-start.1 = ((bf16[4,128,2048]{2,1,0:T(8,128)(2,1)}), bf16[4,128,2048]{2,1,0:T(8,128)(2,1)}, u32[]{:S(2)}, u32[]{:S(2)}) async-start(bf16[4,128,2048]{2,1,0:T(8,128)(2,1)} %bitcast.89), calls=%async_computation.1 | async-start | bytes 4194304 | tf_op jit(solution)/shard_map/all_to_all | solution.py:78
  97.2 5.5 %fusion.5 = f32[512,768]{1,0:T(8,128)} fusion(bf16[512,2048]{1,0:T(8,128)(2,1)} %bitcast.91, bf16[1,2048,768]{2,1,0:T(8,128)(2,1)} %param.13), kind=kOutput, calls=%fused_computation.17 | convolution fusion | flops 1610612736 | bytes 6815744 | tf_op jit(solution)/shard_map/dot_general | solution.py:37
  102.7 41.5 %all-to-all-done.1 = bf16[4,128,2048]{2,1,0:T(8,128)(2,1)} async-done(((bf16[4,128,2048]{2,1,0:T(8,128)(2,1)}), bf16[4,128,2048]{2,1,0:T(8,128)(2,1)}, u32[]{:S(2)}, u32[]{:S(2)}) %all-to-all-start.1) | async-done | bytes 2097184 | tf_op jit(solution)/shard_map/all_to_all | solution.py:78
  148.8 3.2 %multiply_convert_fusion = (bf16[512,768]{1,0:T(8,128)(2,1)}, bf16[512,768]{1,0:T(8,128)(2,1)S(1)}, bf16[512,768]{1,0:T(8,128)(2,1)S(1)}) fusion(f32[512,768]{1,0:T(8,128)S(1)} %copy-done.7, f32[512,768]{1,0:T(8,128)S(1)} %fusion.12, bf16[512,2048]{1,0:T(8,128)(2,1)S(1)} %bitcast.92, bf16[1,2048,768]{2,1,0:T(8,128)(2,1)S(1)} %copy-done), kind=kOutput, calls=%fused_computation.34 | convolution fusion | flops 1616510976 | bytes 10747904 | tf_op jit(solution)/shard_map/dot_general | solution.py:38
  153.1 5.5 %convolution_convert_fusion = bf16[2048,1536]{1,0:T(8,128)(2,1)} fusion(bf16[512,2048]{1,0:T(8,128)(2,1)S(1)} %bitcast.93, bf16[512,768]{1,0:T(8,128)(2,1)S(1)} %get-tuple-element.29, bf16[512,768]{1,0:T(8,128)(2,1)S(1)} %get-tuple-element.28), kind=kOutput, calls=%fused_computation.6 | convolution fusion | flops 3227516928 | bytes 9961472 | tf_op jit(solution)/shard_map/dot_general | solution.py:94
  158.7 4.7 %fusion.1 = bf16[512]{0:T(512)(128)(2,1)S(1)} fusion(bf16[4,128,2048]{2,1,0:T(8,128)(2,1)} %all-to-all-done.1, bf16[512,768]{1,0:T(8,128)(2,1)} %get-tuple-element.27, bf16[1,768,2048]{2,1,0:T(8,128)(2,1)} %param.15), kind=kOutput, calls=%fused_computation.11 | convolution fusion | flops 1613757952 | bytes 6030336 | tf_op jit(solution)/shard_map/dot_general | solution.py:42
  163.9 3.2 %all-to-all-start.4 = ((bf16[1,4,128]{2,0,1:T(2,128)(2,1)}), bf16[1,4,128]{2,0,1:T(2,128)(2,1)S(1)}, u32[]{:S(2)}, u32[]{:S(2)}) async-start(bf16[1,4,128]{2,0,1:T(2,128)(2,1)} %copy.38), calls=%async_computation.4 | async-start | bytes 4096 | tf_op jit(solution)/shard_map/all_to_all | solution.py:121
  169.8 3.6 %convolution_convert_fusion.1 = bf16[768,2048]{1,0:T(8,128)(2,1)} fusion(bf16[512,768]{1,0:T(8,128)(2,1)S(1)} %copy-done.6, bf16[512,2048]{1,0:T(8,128)(2,1)S(1)} %fusion.2), kind=kOutput, calls=%fused_computation.14 | convolution fusion | flops 1612185600 | bytes 6029312 | tf_op jit(solution)/shard_map/dot_general | solution.py:97
  173.5 4.1 %fusion.3 = f32[512,2048]{1,0:T(8,128)S(1)} fusion(bf16[512,768]{1,0:T(8,128)(2,1)} %copy-done.5, bf16[1,2048,768]{2,1,0:T(8,128)(2,1)} %param.13), kind=kOutput, calls=%fused_computation.15 | convolution fusion | flops 1610612736 | bytes 8126464 | tf_op jit(solution)/shard_map/dot_general | solution.py:54
  179.4 5.3 %copy.46 = bf16[1,512,2048]{2,0,1:T(2,128)(2,1)} copy(bf16[1,512,2048]{2,1,0:T(8,128)(2,1)S(1)} %fusion.16) | data formatting | bytes 4194304 | tf_op jit(solution)/shard_map/stack | solution.py:120
  185.1 14.5 %reduce.1 = bf16[512,2048]{1,0:T(8,128)(2,1)} reduce(bf16[512,1,2048]{2,1,0:T(2,128)(2,1)} %bitcast.87, bf16[]{:T(256)} %broadcast.139), dimensions={1}, to_apply=%bitcast.83.reduce_sub_computation | reduce | bytes 4194306
  199.6 4.6 %reshape.245 = bf16[4,2,131072]{2,1,0:T(2,128)(2,1)} reshape(bf16[512,2048]{1,0:T(8,128)(2,1)} %reduce.1) | data formatting | bytes 4194304
  204.2 4.8 %all-to-all-start.3 = ((bf16[4,2,131072]{2,1,0:T(2,128)(2,1)}), bf16[4,2,131072]{2,1,0:T(2,128)(2,1)}, u32[]{:S(2)}, u32[]{:S(2)}) async-start(bf16[4,2,131072]{2,1,0:T(2,128)(2,1)} %reshape.245), calls=%async_computation.3 | async-start | bytes 4194304 | tf_op jit(solution)/shard_map/all_to_all | solution.py:120
  211.9 44.8 %all-to-all-done.3 = bf16[4,2,131072]{2,1,0:T(2,128)(2,1)} async-done(((bf16[4,2,131072]{2,1,0:T(2,128)(2,1)}), bf16[4,2,131072]{2,1,0:T(2,128)(2,1)}, u32[]{:S(2)}, u32[]{:S(2)}) %all-to-all-start.3) | async-done | bytes 2097184 | tf_op jit(solution)/shard_map/all_to_all | solution.py:120
  256.8 5.0 %reshape.246 = bf16[512,1,2048]{2,1,0:T(2,128)(2,1)} reshape(bf16[4,2,131072]{2,1,0:T(2,128)(2,1)} %all-to-all-done.3) | data formatting | bytes 4194304
  261.7 4.9 %copy.45 = bf16[1,512,2048]{2,1,0:T(8,128)(2,1)} copy(bf16[1,512,2048]{2,0,1:T(2,128)(2,1)} %bitcast.88) | data formatting | bytes 4194304
  266.6 5.2 %gather_fusion.1 = bf16[256,2048]{1,0:T(8,128)(2,1)} fusion(bf16[512,2048]{1,0:T(8,128)(2,1)} %bitcast.86, s32[1024]{0:T(1024)S(1)} %pad_clamp_fusion), kind=kCustom, calls=%fused_computation.3 | custom fusion | bytes 2098176 | tf_op jit(solution)/shard_map/jit(_take)/gather | solution.py:130
  274.4 4.4 %fusion.23 = bf16[128,2048]{1,0:T(8,128)(2,1)} fusion(bf16[128,2,2048]{2,1,0:T(2,128)(2,1)} %gather.21, pred[128,2]{1,0:T(8,128)(4,1)S(1)} %get-tuple-element.22), kind=kLoop, calls=%fused_computation.39 | loop fusion | flops 786432 | bytes 1573120 | tf_op jit(solution)/shard_map/reduce_sum | solution.py:131
  (65 shorter events, 25.0 us)
Async XLA Ops:
  7.2 141.4 %copy-start = (bf16[1,2048,768]{2,1,0:T(8,128)(2,1)S(1)}, bf16[1,2048,768]{2,1,0:T(8,128)(2,1)}, u32[]{:S(2)}) copy-start(bf16[1,2048,768]{2,1,0:T(8,128)(2,1)} %param.14) | copy-start | bytes 9437188
  16.6 23.1 %all-to-all-start = ((bf16[4,1,128]{2,1,0:T(2,128)(2,1)}), bf16[4,1,128]{2,1,0:T(2,128)(2,1)S(1)}, u32[]{:S(2)}, u32[]{:S(2)}) async-start(bf16[4,1,128]{2,1,0:T(2,128)(2,1)} %copy.36), calls=%async_computation | async-start | bytes 4096 | tf_op jit(solution)/shard_map/all_to_all | solution.py:79
  92.5 51.7 %all-to-all-start.1 = ((bf16[4,128,2048]{2,1,0:T(8,128)(2,1)}), bf16[4,128,2048]{2,1,0:T(8,128)(2,1)}, u32[]{:S(2)}, u32[]{:S(2)}) async-start(bf16[4,128,2048]{2,1,0:T(8,128)(2,1)} %bitcast.89), calls=%async_computation.1 | async-start | bytes 4194304 | tf_op jit(solution)/shard_map/all_to_all | solution.py:78
  96.9 181.9 %reduce-scatter.3.cloned.1.call-start = ((), (), s32[]{:S(2)}) async-start(), calls=%async_computation.7 | async-start | bytes 7077888 | tf_op jit(solution)/shard_map/reduce_scatter | solution.py:99
  144.2 2.5 copy-start.2
  146.7 1.9 copy-start.1
  146.7 2.0 copy-start.7
  151.9 0.9 copy-start.3
  151.9 1.2 copy-start.5
  163.9 40.2 %all-to-all-start.4 = ((bf16[1,4,128]{2,0,1:T(2,128)(2,1)}), bf16[1,4,128]{2,0,1:T(2,128)(2,1)S(1)}, u32[]{:S(2)}, u32[]{:S(2)}) async-start(bf16[1,4,128]{2,0,1:T(2,128)(2,1)} %copy.38), calls=%async_computation.4 | async-start | bytes 4096 | tf_op jit(solution)/shard_map/all_to_all | solution.py:121
  167.2 113.7 %reduce-scatter.5.cloned.1.call-start = ((), (), s32[]{:S(2)}) async-start(), calls=%async_computation.8 | async-start | bytes 3538944 | tf_op jit(solution)/shard_map/reduce_scatter | solution.py:107
  167.4 2.4 copy-start.6
  173.5 4.1 %copy-start.4 = (bf16[512,768]{1,0:T(8,128)(2,1)S(1)}, bf16[512,768]{1,0:T(8,128)(2,1)}, u32[]{:S(2)}) copy-start(bf16[512,768]{1,0:T(8,128)(2,1)} %copy-done.3) | copy-start | bytes 2359300
  204.2 52.6 %all-to-all-start.3 = ((bf16[4,2,131072]{2,1,0:T(2,128)(2,1)}), bf16[4,2,131072]{2,1,0:T(2,128)(2,1)}, u32[]{:S(2)}, u32[]{:S(2)}) async-start(bf16[4,2,131072]{2,1,0:T(2,128)(2,1)} %reshape.245), calls=%async_computation.3 | async-start | bytes 4194304 | tf_op jit(solution)/shard_map/all_to_all | solution.py:120
Sparse Core Ops, SparseCore 0:
  158.8 60.8 reduce-scatter.2
  223.6 46.0 reduce-scatter.4
where the time goes:
time: 289 us; the launch traced here: 288 us
  waiting for transfers between devices  86.4 us (30%)
  local copies, waits for them, and re-layouts  55.8 us (19%)
  blocking collectives  52.8 us (18%)
  matrix products  30.2 us (10%)
  other arithmetic  28.8 us (10%)
  starting transfers between devices  19.3 us (7%)
  between operations  14.3 us (5%)
    all_to_all x1, blocking collectives, shards(): lax.all_to_all(rows_x, 'expert', split_axis=0, concat_axis=1, tiled=True)  52.8 us
    all_to_all x1, waiting for transfers between devices, shards(): lax.all_to_all(jnp.stack(row_list), 'expert', split_axis=1, concat_axis=0...  44.8 us
    all_to_all x1, waiting for transfers between devices, shards(): lax.all_to_all(rows_dy, 'expert', split_axis=0, concat_axis=1, tiled=True)  41.5 us
    unnamed x23, local copies, waits for them, and re-layouts  19 us
    unnamed x2, other arithmetic  14.5 us
    gather x2, local copies, waits for them, and re-layouts, shards(): picked = jnp.take(flat_rows, dest, axis=0).reshape(tok_rows, top, feature)  7.81 us
    gather x1, local copies, waits for them, and re-layouts, gather_rows(): jnp.take(cotangent, source, axis=0)  6.36 us
    all_to_all x1, starting transfers between devices, shards(): lax.all_to_all(rows_c.astype(jnp.bfloat16), 'expert', split_axis=0, conca...  6.35 us
  transfers between devices with their start and end apart: 6, of which 2 were waited for; matrix products, arithmetic and copies ran while one was open for 32% of the time, Pallas kernels for 0%

commit v1 on v0

v1 whole, which is shorter than its diff:
```python
import jax
import jax.numpy as jnp
from jax import lax
from jax.sharding import PartitionSpec as P


def shards(tokens, cotangent, expert_ids, combine, w_gate, w_up, w_down):
    first = (((0,), (0,)), ((), ()))
    last = (((1,), (1,)), ((), ()))
    local = w_gate.shape[0]
    groups = lax.axis_size("expert")
    experts = local * groups
    rows, top = expert_ids.shape
    hidden_width = w_gate.shape[2]
    names = jnp.arange(experts, dtype=jnp.int32)
    hits = expert_ids[:, :, None] == names
    weight = jnp.sum(jnp.where(hits, combine[:, :, None], 0.0), axis=1)
    weight = lax.all_to_all(weight, "expert", split_axis=1, concat_axis=0, tiled=True)
    x = lax.all_gather(tokens, "expert", axis=0, tiled=True)
    dy = lax.all_gather(cotangent, "expert", axis=0, tiled=True)
    row_sum = 0.0
    combs, gates, ups, downs = [], [], [], []
    for i in range(local):
        w_g, w_u, w_d = w_gate[i], w_up[i], w_down[i]
        gate = jnp.dot(x, w_g, preferred_element_type=jnp.float32)
        up = jnp.dot(x, w_u, preferred_element_type=jnp.float32)
        sig = jax.nn.sigmoid(gate)
        act = gate * sig
        hidden = (act * up).astype(jnp.bfloat16)
        scaled = (weight[:, i : i + 1] * dy.astype(jnp.float32)).astype(jnp.bfloat16)
        output = jnp.dot(hidden, w_d, preferred_element_type=jnp.float32)
        combs.append(jnp.sum(dy.astype(jnp.float32) * output, axis=1))
        hidden_grad = lax.dot_general(scaled, w_d, last, preferred_element_type=jnp.float32)
        gate_d = (hidden_grad * up * (sig * (1.0 + gate * (1.0 - sig)))).astype(jnp.bfloat16)
        up_d = (hidden_grad * act).astype(jnp.bfloat16)
        row = lax.dot_general(gate_d, w_g, last, preferred_element_type=jnp.float32)
        row = row + lax.dot_general(up_d, w_u, last, preferred_element_type=jnp.float32)
        row_sum = row_sum + row.astype(jnp.bfloat16).astype(jnp.float32)
        downs.append(lax.dot_general(hidden, scaled, first, preferred_element_type=jnp.float32))
        gates.append(lax.dot_general(x, gate_d, first, preferred_element_type=jnp.float32))
        ups.append(lax.dot_general(x, up_d, first, preferred_element_type=jnp.float32))

    def reduced(parts):
        return jnp.stack(
            [
                lax.psum_scatter(part.astype(jnp.bfloat16), "dp", scatter_dimension=0, tiled=True)
                for part in parts
            ]
        )

    down_grad = reduced(downs)
    gate_grad = reduced(gates)
    up_grad = reduced(ups)
    input_grad = lax.psum_scatter(
        row_sum.astype(jnp.bfloat16), "expert", scatter_dimension=0, tiled=True
    )
    comb = jnp.stack(combs)
    comb = lax.all_to_all(comb, "expert", split_axis=1, concat_axis=0, tiled=True)
    combine_grad = jnp.sum(jnp.where(hits, comb.T[:, None, :], 0.0), axis=2)
    return (input_grad, combine_grad, gate_grad, up_grad, down_grad)


def solution(mesh):
    by_token = P(("dp", "expert"), None)
    by_expert = P("expert", None, None)
    by_row = P("expert", "dp", None)
    return jax.shard_map(
        shards,
        mesh=mesh,
        in_specs=(by_token,) * 4 + (by_expert,) * 3,
        out_specs=(by_token, by_token, by_row, by_row, by_row),
        check_vma=False,
    )
```

time: 289 us -> 329 us (1.14)
  waiting for transfers between devices: 86.4 us -> 254 us
  local copies, waits for them, and re-layouts: 55.8 us -> 5.92 us
  blocking collectives: 52.8 us -> 15.9 us
  other arithmetic: 28.8 us -> 0.58 us
  starting transfers between devices: 19.3 us -> 0.42 us
  matrix products: 30.2 us -> 37.7 us
    reduce_scatter x2 -> x4, waiting for transfers between devices: 0.01 us -> 166 us  [the longest x3 122 us: reduced(): lax.psum_scatter(part.astype(jnp.bfloat16), 'dp', scatter_dimension=0, ti...]
    all_gather x0 -> x2, waiting for transfers between devices: none -> 86.4 us  [the longest x1 49.3 us: shards(): x = lax.all_gather(tokens, 'expert', axis=0, tiled=True)]
    all_to_all x4 -> x0, waiting for transfers between devices: 86.4 us -> none  [the longest x1 44.8 us: shards(): lax.all_to_all(jnp.stack(row_list), 'expert', split_axis=1, concat_axis=0...]
    all_to_all x1 -> x2, blocking collectives: 52.8 us -> 15.9 us  [the longest x1 8.03 us: shards(): lax.all_to_all(comb, 'expert', split_axis=1, concat_axis=0, tiled=True)]
    gather x7 -> x0, local copies, waits for them, and re-layouts: 26 us -> none  [the longest x2 7.81 us: shards(): picked = jnp.take(flat_rows, dest, axis=0).reshape(tok_rows, top, feature)]
    all_to_all x4 -> x0, starting transfers between devices: 18.8 us -> none  [the longest x1 6.35 us: shards(): lax.all_to_all(rows_c.astype(jnp.bfloat16), 'expert', split_axis=0, conca...]
    unnamed x2 -> x0, other arithmetic: 14.5 us -> none
    unnamed x23 -> x26, local copies, waits for them, and re-layouts: 19 us -> 5.92 us
  transfers between devices with their start and end apart: 6 -> 6, of which waited for: 2 -> 6; matrix products, arithmetic and copies ran while one was open for 32% -> 9% of each run, Pallas kernels for 0% -> 0%
where the time goes in v1:
time: 329 us
  waiting for transfers between devices  254 us (77%)
  matrix products  37.7 us (11%)
  blocking collectives  15.9 us (5%)
  between operations  14.2 us (4%)
  local copies, waits for them, and re-layouts  5.92 us (2%)
    reduce_scatter x3, waiting for transfers between devices, reduced(): lax.psum_scatter(part.astype(jnp.bfloat16), 'dp', scatter_dimension=0, ti...  122 us
    all_gather x1, waiting for transfers between devices, shards(): x = lax.all_gather(tokens, 'expert', axis=0, tiled=True)  49.3 us
    reduce_scatter x1, waiting for transfers between devices, shards(): lax.psum_scatter(row_sum.astype(jnp.bfloat16), 'expert', scatter_dimensio...  44.4 us
    all_gather x1, waiting for transfers between devices, shards(): dy = lax.all_gather(cotangent, 'expert', axis=0, tiled=True)  37.2 us
    all_to_all x1, blocking collectives, shards(): lax.all_to_all(comb, 'expert', split_axis=1, concat_axis=0, tiled=True)  8.03 us
    all_to_all x1, blocking collectives, shards(): lax.all_to_all(weight, 'expert', split_axis=1, concat_axis=0, tiled=True)  7.9 us
  transfers between devices with their start and end apart: 6, of which 6 were waited for; matrix products, arithmetic and copies ran while one was open for 9% of the time, Pallas kernels for 0%

profile of v1, /device:TPU:0, one launch (start us, length us, event | category | flops | bytes accessed | tf_op | source)
XLA Modules:
  0.0 329.0 jit_solution(15756444999730954706)
XLA Ops:
  7.2 0.7 all-gather.5.cloned.1.call-update
  8.0 0.7 all-gather.3.cloned.1.call-update
  8.7 49.3 %all-gather.5.cloned.1.call-done = bf16[512,2048]{1,0:T(8,128)(2,1)} async-done(((bf16[128,2048]{1,0:T(8,128)(2,1)}), bf16[512,2048]{1,0:T(8,128)(2,1)}) %all-gather.5.cloned.1.call-update) | async-done | bytes 2097168 | tf_op jit(solution)/shard_map/all_gather | solution.py:19
  58.0 4.5 %fusion.4 = f32[512,768]{1,0:T(8,128)S(1)} fusion(bf16[512,2048]{1,0:T(8,128)(2,1)} %all-gather.5.cloned.1.call-done, bf16[1,2048,768]{2,1,0:T(8,128)(2,1)} %param.11), kind=kOutput, calls=%fused_computation.10 | convolution fusion | flops 1610612736 | bytes 6815744 | tf_op jit(solution)/shard_map/dot_general | solution.py:25
  62.4 1.2 copy-done.9
  63.6 3.2 multiply_convert_fusion
  66.9 37.2 %all-gather.3.cloned.1.call-done = bf16[512,2048]{1,0:T(8,128)(2,1)} async-done(((bf16[128,2048]{1,0:T(8,128)(2,1)}), bf16[512,2048]{1,0:T(8,128)(2,1)}) %all-gather.3.cloned.1.call-update) | async-done | bytes 2097168 | tf_op jit(solution)/shard_map/all_gather | solution.py:20
  104.1 4.8 %fusion.1 = f32[512]{0:T(512)S(1)} fusion(bf16[512,2048]{1,0:T(8,128)(2,1)} %all-gather.3.cloned.1.call-done, bf16[512,768]{1,0:T(8,128)(2,1)} %get-tuple-element.29, bf16[1,768,2048]{2,1,0:T(8,128)(2,1)} %param.13), kind=kOutput, calls=%fused_computation.3 | convolution fusion | flops 1613757952 | bytes 6031360 | tf_op jit(solution)/shard_map/dot_general | solution.py:31
  108.9 8.0 %all_to_all.32 = f32[1,4,128]{2,0,1:T(1,128)S(1)} all-to-all(f32[1,4,128]{2,0,1:T(1,128)S(1)} %bitcast.56), channel_id=1, replica_groups=mesh['dp'=8,'expert'=4] {'expert'}, dimensions={1} | all-to-all | bytes 4096 | tf_op jit(solution)/shard_map/all_to_all | solution.py:58
  116.9 0.6 select_reduce_fusion
  117.5 7.9 %all_to_all.33 = f32[128,4,1]{0,2,1:T(1,128)S(1)} all-to-all(f32[128,4,1]{0,2,1:T(1,128)S(1)} %bitcast.53), channel_id=1, replica_groups=mesh['dp'=8,'expert'=4] {'expert'}, dimensions={1} | all-to-all | bytes 4096 | tf_op jit(solution)/shard_map/all_to_all | solution.py:18
  125.4 3.3 multiply_convert_fusion.1
  128.7 0.9 copy-done.7
  129.6 3.5 %fusion.14 = bf16[2048,768]{0,1:T(8,128)(2,1)} fusion(bf16[512,768]{1,0:T(8,128)(2,1)S(1)} %get-tuple-element.27, bf16[512,2048]{1,0:T(8,128)(2,1)S(1)} %copy-done.6), kind=kOutput, calls=%fused_computation.20 | convolution fusion | flops 1612185600 | bytes 6029312 | tf_op jit(solution)/shard_map/dot_general | solution.py:41
  133.2 5.3 %fusion.13 = bf16[2048,768]{0,1:T(8,128)(2,1)} fusion(bf16[512,768]{1,0:T(8,128)(2,1)} %get-tuple-element.28, bf16[512,2048]{1,0:T(8,128)(2,1)} %all-gather.5.cloned.1.call-done), kind=kOutput, calls=%fused_computation.19 | convolution fusion | flops 1612185600 | bytes 6029312 | tf_op jit(solution)/shard_map/dot_general | solution.py:40
  138.7 4.3 %fusion.2 = f32[512,2048]{1,0:T(8,128)S(1)} fusion(bf16[512,768]{1,0:T(8,128)(2,1)} %get-tuple-element.28, bf16[1,2048,768]{2,1,0:T(8,128)(2,1)} %param.11), kind=kOutput, calls=%fused_computation.8 | convolution fusion | flops 1610612736 | bytes 8126464 | tf_op jit(solution)/shard_map/dot_general | solution.py:36
  143.1 3.3 add_convert_fusion
  146.4 5.5 %convolution_convert_fusion = bf16[768,2048]{1,0:T(8,128)(2,1)} fusion(bf16[512,768]{1,0:T(8,128)(2,1)} %get-tuple-element.29, bf16[512,2048]{1,0:T(8,128)(2,1)} %all-gather.3.cloned.1.call-done, f32[512]{0:T(512)S(1)} %bitcast.55), kind=kOutput, calls=%fused_computation.5 | convolution fusion | flops 1615331328 | bytes 6031360 | tf_op jit(solution)/shard_map/dot_general | solution.py:39
  151.9 25.5 %reduce-scatter.9.cloned.1.call-done = bf16[256,768]{0,1:T(8,128)(2,1)} async-done(((bf16[2048,768]{0,1:T(8,128)(2,1)}), bf16[256,768]{0,1:T(8,128)(2,1)}) %reduce-scatter.9.cloned.1.call-update) | async-done | bytes 393232 | tf_op jit(solution)/shard_map/reduce_scatter | solution.py:46
  177.4 1.9 copy.30
  179.3 47.4 %reduce-scatter.7.cloned.1.call-done = bf16[256,768]{0,1:T(8,128)(2,1)} async-done(((bf16[2048,768]{0,1:T(8,128)(2,1)}), bf16[256,768]{0,1:T(8,128)(2,1)}) %reduce-scatter.7.cloned.1.call-update) | async-done | bytes 393232 | tf_op jit(solution)/shard_map/reduce_scatter | solution.py:46
  226.7 1.9 copy.29
  228.6 44.4 %reduce-scatter.5.cloned.1.call-done = bf16[128,2048]{1,0:T(8,128)(2,1)} async-done(((bf16[512,2048]{1,0:T(8,128)(2,1)}), bf16[128,2048]{1,0:T(8,128)(2,1)}) %reduce-scatter.5.cloned.1.call-update) | async-done | bytes 524304 | tf_op jit(solution)/shard_map/reduce_scatter | solution.py:54
  273.0 49.1 %reduce-scatter.11.cloned.1.call-done = bf16[96,2048]{1,0:T(8,128)(2,1)} async-done(((bf16[768,2048]{1,0:T(8,128)(2,1)}), bf16[96,2048]{1,0:T(8,128)(2,1)}) %reduce-scatter.11.cloned.1.call-update) | async-done | bytes 393232 | tf_op jit(solution)/shard_map/reduce_scatter | solution.py:46
  (32 shorter events, 0.5 us)
Async XLA Ops:
  7.2 56.4 %copy-start = (bf16[1,2048,768]{2,1,0:T(8,128)(2,1)S(1)}, bf16[1,2048,768]{2,1,0:T(8,128)(2,1)}, u32[]{:S(2)}) copy-start(bf16[1,2048,768]{2,1,0:T(8,128)(2,1)} %param.12) | copy-start | bytes 9437188
  7.2 50.8 %all-gather.5.cloned.1.call-start = ((), (), s32[]{:S(2)}) async-start(), calls=%async_computation.7 | async-start | bytes 2621440 | tf_op jit(solution)/shard_map/all_gather | solution.py:19
  7.9 96.1 %all-gather.3.cloned.1.call-start = ((), (), s32[]{:S(2)}) async-start(), calls=%async_computation.6 | async-start | bytes 2621440 | tf_op jit(solution)/shard_map/all_gather | solution.py:20
  8.7 168.7 %reduce-scatter.9.cloned.1.call-start = ((), (), s32[]{:S(2)}) async-start(), calls=%async_computation.10 | async-start | bytes 3538944 | tf_op jit(solution)/shard_map/reduce_scatter | solution.py:46
  58.0 5.6 %copy-start.5 = (bf16[512,2048]{1,0:T(8,128)(2,1)S(1)}, bf16[512,2048]{1,0:T(8,128)(2,1)}, u32[]{:S(2)}) copy-start(bf16[512,2048]{1,0:T(8,128)(2,1)} %all-gather.5.cloned.1.call-done) | copy-start | bytes 6291460
  62.4 1.2 copy-start.9
  104.0 12.9 %copy-start.1 = (s32[128,2]{0,1:T(2,128)S(1)}, s32[128,2]{0,1:T(2,128)}, u32[]{:S(2)}) copy-start(s32[128,2]{0,1:T(2,128)} %param.9) | copy-start | bytes 3076
  104.0 12.9 %copy-start.2 = (f32[128,2]{0,1:T(2,128)S(1)}, f32[128,2]{0,1:T(2,128)}, u32[]{:S(2)}) copy-start(f32[128,2]{0,1:T(2,128)} %param.10) | copy-start | bytes 3076
  104.0 21.3 %copy-start.3 = (bf16[1,768,2048]{2,1,0:T(8,128)(2,1)S(1)}, bf16[1,768,2048]{2,1,0:T(8,128)(2,1)}, u32[]{:S(2)}) copy-start(bf16[1,768,2048]{2,1,0:T(8,128)(2,1)} %param.13) | copy-start | bytes 9437188
  104.0 21.3 %copy-start.4 = (bf16[512,2048]{1,0:T(8,128)(2,1)S(1)}, bf16[512,2048]{1,0:T(8,128)(2,1)}, u32[]{:S(2)}) copy-start(bf16[512,2048]{1,0:T(8,128)(2,1)} %all-gather.3.cloned.1.call-done) | copy-start | bytes 6291460
  104.0 21.3 %copy-start.10 = (f32[512,768]{1,0:T(8,128)S(1)}, f32[512,768]{1,0:T(8,128)}, u32[]{:S(2)}) copy-start(f32[512,768]{1,0:T(8,128)} %copy-done.9) | copy-start | bytes 4718596
  104.0 21.3 %copy-start.11 = (f32[512,768]{1,0:T(8,128)S(1)}, f32[512,768]{1,0:T(8,128)}, u32[]{:S(2)}) copy-start(f32[512,768]{1,0:T(8,128)} %get-tuple-element.30) | copy-start | bytes 4718596
  125.4 4.2 %copy-start.6 = (bf16[512,2048]{1,0:T(8,128)(2,1)S(1)}, bf16[512,2048]{1,0:T(8,128)(2,1)}, u32[]{:S(2)}) copy-start(bf16[512,2048]{1,0:T(8,128)(2,1)} %all-gather.5.cloned.1.call-done) | copy-start | bytes 6291460
  128.7 0.9 copy-start.7
  133.1 93.6 %reduce-scatter.7.cloned.1.call-start = ((), (), s32[]{:S(2)}) async-start(), calls=%async_computation.9 | async-start | bytes 3538944 | tf_op jit(solution)/shard_map/reduce_scatter | solution.py:46
  138.5 134.5 %reduce-scatter.5.cloned.1.call-start = ((), (), s32[]{:S(2)}) async-start(), calls=%async_computation.8 | async-start | bytes 2621440 | tf_op jit(solution)/shard_map/reduce_scatter | solution.py:54
  138.7 4.3 %copy-start.8 = (bf16[512,768]{1,0:T(8,128)(2,1)S(1)}, bf16[512,768]{1,0:T(8,128)(2,1)}, u32[]{:S(2)}) copy-start(bf16[512,768]{1,0:T(8,128)(2,1)} %copy-done.7) | copy-start | bytes 2359300
  146.4 175.8 %reduce-scatter.11.cloned.1.call-start = ((), (), s32[]{:S(2)}) async-start(), calls=%async_computation.11 | async-start | bytes 3538944 | tf_op jit(solution)/shard_map/reduce_scatter | solution.py:46
Sparse Core Ops, SparseCore 0:
  9.6 48.3 all-gather.4
  59.5 44.4 all-gather.2
  133.2 44.0 reduce-scatter.8
  180.6 46.0 reduce-scatter.6
  229.4 43.5 reduce-scatter.4
  276.8 45.2 reduce-scatter.10

commit v2 on v1

v2 whole, which is shorter than its diff:
```python
import functools
import jax
import jax.numpy as jnp
from jax import lax
from jax.experimental import pallas as pl
from jax.experimental.pallas import tpu as pltpu
from jax.sharding import PartitionSpec as P

MESH = pl.DeviceIdType.MESH
VMEM = pl.BlockSpec(memory_space=pltpu.VMEM)
LIMIT = 56 * 1024 * 1024


def remote(src, dst, send, recv, axis, target):
    return pltpu.make_async_remote_copy(
        src_ref=src,
        dst_ref=dst,
        send_sem=send,
        recv_sem=recv,
        device_id={axis: target},
        device_id_type=MESH,
    )


def gather_kernel(n, x, dy, w, x_all, dy_all, w_all, send, recv, w_send, w_recv):
    me = lax.axis_index("expert")
    barrier = pltpu.get_barrier_semaphore()
    for k in range(1, n):
        pl.semaphore_signal(
            barrier, inc=1, device_id={"expert": lax.rem(me + k, n)}, device_id_type=MESH
        )
    pl.semaphore_wait(barrier, n - 1)

    def hop(t, side, s):
        own, full = ((x, x_all), (dy, dy_all))[t]
        step = 1 if side == 0 else -1
        block = jnp.clip(me - step * s, 0, n - 1)
        src = own if s == 0 else full.at[block]
        target = jnp.clip(me + step, 0, n - 1)
        return remote(
            src, full.at[block], send.at[t, side, s], recv.at[t, side, s], "expert", target
        )

    def arrival(t, side, s):
        full = (x_all, dy_all)[t]
        step = 1 if side == 0 else -1
        block = jnp.clip(me - step * (s + 1), 0, n - 1)
        slot = full.at[block]
        return remote(slot, slot, send.at[t, side, s], recv.at[t, side, s], "expert", me)

    def sends(side, s):
        if side == 0:
            return jnp.logical_and(me >= s, me + 1 < n)
        return jnp.logical_and(me + s < n, me >= 1)

    def gets(side, s):
        return me >= s + 1 if side == 0 else me + s + 1 < n

    for t in range(2):
        for s in range(n):
            for side in range(2):
                if s >= 1:

                    @pl.when(gets(side, s - 1))
                    def _():
                        arrival(t, side, s - 1).wait_recv()

                if s < n - 1:

                    @pl.when(sends(side, s))
                    def _():
                        hop(t, side, s).start()

            if s == 0:
                if t == 0:
                    small = []
                    for k in range(1, n):
                        small.append(
                            remote(
                                w,
                                w_all.at[k],
                                w_send.at[k],
                                w_recv.at[k],
                                "expert",
                                lax.rem(me + k, n),
                            )
                        )
                        small[-1].start()
                    x_all[me] = x[...]
                    dy_all[me] = dy[...]
                    w_all[0] = w[...]
    for t in range(2):
        for s in range(n - 1):
            for side in range(2):

                @pl.when(sends(side, s))
                def _():
                    hop(t, side, s).wait_send()

    for copy in small:
        copy.wait()


def gather_all(n, x, dy, w):
    outs = [jax.ShapeDtypeStruct((n,) + a.shape, a.dtype) for a in (x, dy, w)]
    return pl.pallas_call(
        functools.partial(gather_kernel, n),
        out_shape=outs,
        in_specs=[VMEM] * 3,
        out_specs=[VMEM] * 3,
        scratch_shapes=[
            pltpu.SemaphoreType.DMA((2, 2, n)),
            pltpu.SemaphoreType.DMA((2, 2, n)),
            pltpu.SemaphoreType.DMA((n,)),
            pltpu.SemaphoreType.DMA((n,)),
        ],
        compiler_params=pltpu.CompilerParams(
            collective_id=0, has_side_effects=True, vmem_limit_bytes=LIMIT
        ),
        name="gather_all",
    )(x, dy, w)


def reduce_kernel(n, bits, *refs):
    rows, comb, both, down, in_grad, comb_all, gate_out, up_out, down_out = refs[:9]
    got_rows, r_send, r_recv, c_send, c_recv = refs[9:14]
    rest = refs[14:]
    gots = [rest[2 * p : 2 * p + 2] for p in range(bits)]
    sums = [rest[2 * bits + 2 * p : 2 * bits + 2 * p + 2] for p in range(bits - 1)]
    send, recv = rest[-2:]
    me = lax.axis_index("expert")
    rank = lax.axis_index("dp")
    bit = [lax.rem(rank // (1 << b), 2) for b in range(bits)]
    mate = [rank + (1 - 2 * bit[b]) * (1 << b) for b in range(bits)]
    barrier = pltpu.get_barrier_semaphore()
    for k in range(1, n):
        pl.semaphore_signal(
            barrier, inc=1, device_id={"expert": lax.rem(me + k, n)}, device_id_type=MESH
        )
    for b in range(bits):
        pl.semaphore_signal(barrier, inc=1, device_id={"dp": mate[b]}, device_id_type=MESH)
    pl.semaphore_wait(barrier, n - 1 + bits)

    orders = ([0] + list(range(1, bits)), [0] + list(range(bits - 1, 0, -1)))
    inputs = (both, down)

    def span(a, h):
        half = inputs[a].shape[2] // 2
        return pl.ds(h * half, half)

    def block_of(order, value, m):
        block = value * (1 << order[0])
        for i, b in enumerate(order[1:]):
            block = block + lax.rem(m // (1 << i), 2) * (1 << b)
        return block

    def copy(p, h, a, m):
        order = orders[h]
        b = order[p]
        if p == 0:
            src = inputs[a].at[block_of(order, 1 - bit[b], m), :, span(a, h)]
        else:
            src = sums[p - 1][a].at[h, 1 - bit[b] + 2 * m]
        return remote(
            src, gots[p][a].at[h, m], send.at[p, h, a, m], recv.at[p, h, a, m], "dp", mate[b]
        )

    def slots(p, h):
        count = 1 << (bits - 1 - p)
        if count == 1:
            return [(0, None)]
        lead = bit[orders[h][p + 1]]
        going = [(1 - lead + 2 * k, k) for k in range(count // 2)]
        return going + [(lead + 2 * k, None) for k in range(count // 2)]

    for h in range(2):
        for m, _ in slots(0, h):
            for a in range(2):
                copy(0, h, a, m).start()
    exchange = []
    for k in range(1, n):
        target = lax.rem(me + k, n)
        exchange.append(
            remote(rows.at[target], got_rows.at[k], r_send.at[k], r_recv.at[k], "expert", target)
        )
        exchange.append(
            remote(comb.at[target], comb_all.at[k], c_send.at[k], c_recv.at[k], "expert", target)
        )
    for item in exchange:
        item.start()
    comb_all[0] = comb[me]

    for p in range(bits):
        plans = [slots(p, h) for h in range(2)]
        for i in range(len(plans[0])):
            for h in range(2):
                m, onward = plans[h][i]
                order = orders[h]
                mine = bit[order[p]]
                for a in range(2):
                    copy(p, h, a, m).wait_recv()
                    if p == 0:
                        held = inputs[a][block_of(order, mine, m), :, span(a, h)]
                    else:
                        held = sums[p - 1][a][h, mine + 2 * m]
                    total = held.astype(jnp.float32) + gots[p][a][h, m].astype(jnp.float32)
                    total = total.astype(jnp.bfloat16)
                    if p < bits - 1:
                        sums[p][a][h, m] = total
                        if onward is not None:
                            copy(p + 1, h, a, onward).start()
                    elif a == 0:
                        (gate_out, up_out)[h][...] = total
                    else:
                        down_out[:, span(a, h)] = total
    for item in exchange:
        item.wait_recv()
    summed = rows[me].astype(jnp.float32)
    for k in range(1, n):
        summed = summed + got_rows[k].astype(jnp.float32)
    in_grad[...] = summed.astype(jnp.bfloat16)
    for item in exchange:
        item.wait_send()
    for p in range(bits):
        for h in range(2):
            for m, _ in slots(p, h):
                for a in range(2):
                    copy(p, h, a, m).wait_send()


def reduce_all(n, replicas, rows, comb, both, down):
    bits = replicas.bit_length() - 1
    width = both.shape[2] // 2
    bf16 = jnp.bfloat16
    outs = [
        jax.ShapeDtypeStruct(rows.shape[1:], bf16),
        jax.ShapeDtypeStruct(comb.shape, jnp.float32),
        jax.ShapeDtypeStruct((both.shape[1], width), bf16),
        jax.ShapeDtypeStruct((both.shape[1], width), bf16),
        jax.ShapeDtypeStruct(down.shape[1:], bf16),
    ]
    halves = [(a.shape[1], a.shape[2] // 2) for a in (both, down)]
    scratch = [pltpu.VMEM(rows.shape, bf16)]
    scratch += [pltpu.SemaphoreType.DMA((n,))] * 4
    for phases in (bits, bits - 1):
        for p in range(phases):
            scratch += [pltpu.VMEM((2, 1 << (bits - 1 - p)) + half, bf16) for half in halves]
    scratch += [pltpu.SemaphoreType.DMA((bits, 2, 2, 1 << (bits - 1)))] * 2
    return pl.pallas_call(
        functools.partial(reduce_kernel, n, bits),
        out_shape=outs,
        in_specs=[VMEM] * 4,
        out_specs=[VMEM] * 5,
        scratch_shapes=scratch,
        compiler_params=pltpu.CompilerParams(
            collective_id=1, has_side_effects=True, vmem_limit_bytes=LIMIT
        ),
        name="reduce_all",
    )(rows, comb, both, down)


def shards(tokens, cotangent, expert_ids, combine, w_gate, w_up, w_down):
    first = (((0,), (0,)), ((), ()))
    last = (((1,), (1,)), ((), ()))
    groups = lax.axis_size("expert")
    replicas = lax.axis_size("dp")
    me = lax.axis_index("expert")
    rows, top = expert_ids.shape
    feature = tokens.shape[1]
    hidden_width = w_gate.shape[2]
    names = jnp.arange(groups, dtype=jnp.int32)
    hits = expert_ids[:, :, None] == names
    weight = jnp.sum(jnp.where(hits, combine[:, :, None], 0.0), axis=1)
    table = jnp.pad(weight.T, ((0, -groups % 8), (0, 0)))
    x, dy, tables = gather_all(groups, tokens, cotangent, table)
    x = x.reshape(groups * rows, feature)
    dy = dy.reshape(groups * rows, feature)
    sources = lax.rem(me - names + groups, groups)
    mine = lax.dynamic_index_in_dim(tables, me, axis=1, keepdims=False)
    coeff = mine[sources].reshape(groups * rows, 1)
    w_g, w_u, w_d = w_gate[0], w_up[0], w_down[0]
    gate = jnp.dot(x, w_g, preferred_element_type=jnp.float32)
    up = jnp.dot(x, w_u, preferred_element_type=jnp.float32)
    sig = jax.nn.sigmoid(gate)
    act = gate * sig
    hidden = (act * up).astype(jnp.bfloat16)
    scaled = (coeff * dy.astype(jnp.float32)).astype(jnp.bfloat16)
    output = jnp.dot(hidden, w_d, preferred_element_type=jnp.float32)
    comb = jnp.sum(dy.astype(jnp.float32) * output, axis=1)
    hidden_grad = lax.dot_general(scaled, w_d, last, preferred_element_type=jnp.float32)
    gate_d = (hidden_grad * up * (sig * (1.0 + gate * (1.0 - sig)))).astype(jnp.bfloat16)
    up_d = (hidden_grad * act).astype(jnp.bfloat16)
    row = lax.dot_general(gate_d, w_g, last, preferred_element_type=jnp.float32)
    row = row + lax.dot_general(up_d, w_u, last, preferred_element_type=jnp.float32)
    row = row.astype(jnp.bfloat16).reshape(groups, rows, feature)
    paired = jnp.concatenate([gate_d, up_d], axis=1)
    both = lax.dot_general(x, paired, first, preferred_element_type=jnp.float32)
    both = both.astype(jnp.bfloat16).reshape(replicas, feature // replicas, 2 * hidden_width)
    down = lax.dot_general(hidden, scaled, first, preferred_element_type=jnp.float32)
    down = down.astype(jnp.bfloat16).reshape(replicas, hidden_width // replicas, feature)
    comb = jnp.broadcast_to(comb.reshape(groups, 1, rows), (groups, 8, rows))
    input_grad, combs, gate_grad, up_grad, down_grad = reduce_all(
        groups, replicas, row, comb, both, down
    )
    comb = combs[sources, 0]
    combine_grad = jnp.sum(jnp.where(hits, comb.T[:, None, :], 0.0), axis=2)
    return (input_grad, combine_grad, gate_grad[None], up_grad[None], down_grad[None])


def solution(mesh):
    by_token = P(("dp", "expert"), None)
    by_expert = P("expert", None, None)
    by_row = P("expert", "dp", None)
    return jax.shard_map(
        shards,
        mesh=mesh,
        in_specs=(by_token,) * 4 + (by_expert,) * 3,
        out_specs=(by_token, by_token, by_row, by_row, by_row),
        check_vma=False,
    )
```

time: 329 us -> 171 us (0.52)
  waiting for transfers between devices: 254 us -> 0 us
  Pallas kernels: 0 us -> 130 us
  blocking collectives: 15.9 us -> 0 us
  between operations: 14.2 us -> 0.77 us
  matrix products: 37.7 us -> 25.7 us
  local copies, waits for them, and re-layouts: 5.92 us -> 9.52 us
  other arithmetic: 0.58 us -> 4.01 us
    reduce_scatter x4 -> x0, waiting for transfers between devices: 166 us -> none  [the longest x3 122 us: reduced(): lax.psum_scatter(part.astype(jnp.bfloat16), 'dp', scatter_dimension=0, ti...]
    pallas_call x0 -> x2, Pallas kernels: none -> 130 us  [the longest x1 78.3 us: gather_all(): pl.pallas_call(functools.partial(gather_kernel, n), out_shape=outs, in_sp...]
    all_gather x2 -> x0, waiting for transfers between devices: 86.4 us -> none  [the longest x1 49.3 us: shards(): x = lax.all_gather(tokens, 'expert', axis=0, tiled=True)]
    all_to_all x2 -> x0, blocking collectives: 15.9 us -> none  [the longest x1 8.03 us: shards(): lax.all_to_all(comb, 'expert', split_axis=1, concat_axis=0, tiled=True)]
    dot_general x2 -> x1, matrix products: 8.82 us -> 5.63 us  [shards(): both = lax.dot_general(x, paired, first, preferred_element_type=jnp.float32)]
  transfers between devices with their start and end apart: 6 -> 0, of which waited for: 6 -> 0; matrix products, arithmetic and copies ran while one was open for 9% -> 0% of each run, Pallas kernels for 0% -> 0%
where the time goes in v2:
time: 171 us; the launch traced here: 170 us
  Pallas kernels  130 us (76%)
  matrix products  25.7 us (15%)
  local copies, waits for them, and re-layouts  9.52 us (6%)
  other arithmetic  4.01 us (2%)
    pallas_call x1, Pallas kernels, gather_all(): pl.pallas_call(functools.partial(gather_kernel, n), out_shape=outs, in_sp...  78.3 us
    pallas_call x1, Pallas kernels, reduce_all(): pl.pallas_call(functools.partial(reduce_kernel, n, bits), out_shape=outs,...  51.9 us
    unnamed x22, local copies, waits for them, and re-layouts  5.69 us
    dot_general x1, matrix products, shards(): both = lax.dot_general(x, paired, first, preferred_element_type=jnp.float32)  5.63 us
    dot_general x1, matrix products, shards(): gate = jnp.dot(x, w_g, preferred_element_type=jnp.float32)  5.49 us
    dot_general x1, matrix products, shards(): lax.dot_general(hidden, scaled, first, preferred_element_type=jnp.float32)  3.54 us

profile of v2, /device:TPU:0, one launch (start us, length us, event | category | flops | bytes accessed | tf_op | source)
XLA Modules:
  0.0 170.2 jit_solution(9103448196710936432)
XLA Ops:
  0.6 0.9 select_reduce_fusion.1
  1.5 0.6 pad.5.w
  2.1 78.3 %gather_all.1 = (bf16[4,128,2048]{2,1,0:T(8,128)(2,1)}, bf16[4,128,2048]{2,1,0:T(8,128)(2,1)}, f32[4,8,128]{2,1,0:T(8,128)}) custom-call(bf16[128,2048]{1,0:T(8,128)(2,1)} %x.5, bf16[128,2048]{1,0:T(8,128)(2,1)} %dy.1, f32[8,128]{1,0:T(8,128)} %pad.5.w), custom_call_target="tpu_custom_call" | custom-call | tf_op jit(solution)/shard_map/gather_all/pallas_call | solution.py:106
  80.4 5.5 %fusion.5 = f32[512,768]{1,0:T(8,128)} fusion(bf16[512,2048]{1,0:T(8,128)(2,1)} %bitcast.64, bf16[1,2048,768]{2,1,0:T(8,128)(2,1)} %param.11), kind=kOutput, calls=%fused_computation.13 | convolution fusion | flops 1610612736 | bytes 6815744 | tf_op jit(solution)/shard_map/dot_general | solution.py:282
  85.9 0.7 constant_dynamic-slice_fusion
  86.6 0.6 gather_fusion
  87.2 2.1 %fusion = bf16[4,128,2048]{2,1,0:T(8,128)(2,1)S(1)} fusion(bf16[4,128,2048]{2,1,0:T(8,128)(2,1)} %get-tuple-element.14, f32[4,128]{1,0:T(4,128)S(1)} %gather_fusion), kind=kLoop, calls=%fused_computation.6 | loop fusion | flops 3145728 | bytes 4196352 | tf_op jit(solution)/shard_map/convert_element_type | solution.py:287
  89.3 0.4 copy-done.6
  89.7 1.9 %fusion.12 = f32[512,768]{1,0:T(8,128)S(1)} fusion(bf16[512,2048]{1,0:T(8,128)(2,1)S(1)} %bitcast.54, bf16[1,768,2048]{2,1,0:T(8,128)(2,1)S(1)} %copy-done.6), kind=kOutput, calls=%fused_computation.20 | convolution fusion | flops 1610612736 | bytes 6815744 | tf_op jit(solution)/shard_map/dot_general | solution.py:290
  91.8 2.3 %multiply_convert_fusion = (bf16[512,768]{1,0:T(8,128)(2,1)S(1)}, bf16[512,768]{1,0:T(8,128)(2,1)S(1)}, bf16[512,768]{1,0:T(8,128)(2,1)S(1)}) fusion(f32[512,768]{1,0:T(8,128)S(1)} %copy-done.8, f32[512,768]{1,0:T(8,128)S(1)} %fusion.12, bf16[512,2048]{1,0:T(8,128)(2,1)S(1)} %bitcast.65, bf16[1,2048,768]{2,1,0:T(8,128)(2,1)S(1)} %copy-done), kind=kOutput, calls=%fused_computation.25 | convolution fusion | flops 1616510976 | bytes 10747904 | tf_op jit(solution)/shard_map/dot_general | solution.py:283
  94.0 1.8 %fusion.3 = f32[512,2048]{1,0:T(8,128)S(1)} fusion(bf16[512,768]{1,0:T(8,128)(2,1)S(1)} %get-tuple-element.22, bf16[1,2048,768]{2,1,0:T(8,128)(2,1)S(1)} %copy-done.5), kind=kOutput, calls=%fused_computation.11 | convolution fusion | flops 1610612736 | bytes 8126464 | tf_op jit(solution)/shard_map/dot_general | solution.py:293
  95.9 3.2 %add_convert_fusion = bf16[512,2048]{1,0:T(8,128)(2,1)} fusion(f32[512,2048]{1,0:T(8,128)S(1)} %fusion.3, bf16[512,768]{1,0:T(8,128)(2,1)S(1)} %get-tuple-element.23, bf16[1,2048,768]{2,1,0:T(8,128)(2,1)S(1)} %copy-done), kind=kOutput, calls=%fused_computation.9 | convolution fusion | flops 1612709888 | bytes 10223616 | tf_op jit(solution)/shard_map/dot_general | solution.py:294
  99.0 2.0 %fusion.1 = f32[512]{0:T(512)S(1)} fusion(bf16[4,128,2048]{2,1,0:T(8,128)(2,1)S(1)} %copy-done.1, bf16[512,768]{1,0:T(8,128)(2,1)S(1)} %get-tuple-element.21, bf16[1,768,2048]{2,1,0:T(8,128)(2,1)S(1)} %copy-done.6), kind=kOutput, calls=%fused_computation.7 | convolution fusion | flops 1613757952 | bytes 6031360 | tf_op jit(solution)/shard_map/dot_general | solution.py:288
  101.0 0.6 broadcast_in_dim.47.refs_1_
  101.6 5.6 %convolution_convert_fusion = bf16[2048,1536]{1,0:T(8,128)(2,1)} fusion(bf16[512,2048]{1,0:T(8,128)(2,1)S(1)} %bitcast.66, bf16[512,768]{1,0:T(8,128)(2,1)S(1)} %get-tuple-element.23, bf16[512,768]{1,0:T(8,128)(2,1)S(1)} %get-tuple-element.22), kind=kOutput, calls=%fused_computation.2 | convolution fusion | flops 3227516928 | bytes 9961472 | tf_op jit(solution)/shard_map/dot_general | solution.py:297
  107.2 0.4 fusion.2
  107.7 3.5 %convolution_convert_fusion.1 = bf16[768,2048]{1,0:T(8,128)(2,1)} fusion(bf16[512,768]{1,0:T(8,128)(2,1)S(1)} %get-tuple-element.21, bf16[512,2048]{1,0:T(8,128)(2,1)S(1)} %fusion.2), kind=kOutput, calls=%fused_computation.10 | convolution fusion | flops 1612185600 | bytes 6029312 | tf_op jit(solution)/shard_map/dot_general | solution.py:299
  111.2 51.9 %reduce_all.1 = (bf16[128,2048]{1,0:T(8,128)(2,1)}, f32[4,8,128]{2,1,0:T(8,128)}, bf16[256,768]{1,0:T(8,128)(2,1)}, bf16[256,768]{1,0:T(8,128)(2,1)}, bf16[96,2048]{1,0:T(8,128)(2,1)}) custom-call(bf16[4,128,2048]{2,1,0:T(8,128)(2,1)} %bitcast.55, f32[4,8,128]{2,1,0:T(8,128)} %broadcast_in_dim.47.refs_1_, bf16[8,256,1536]{2,1,0:T(8,128)(2,1)} %bitcast.52, ...), custom_call_target="tpu_custom_call" | custom-call | tf_op jit(solution)/shard_map/reduce_all/pallas_call | solution.py:249
  163.1 1.3 gather_fusion.1
  164.5 0.6 select_reduce_fusion
  165.1 1.9 %copy.19 = bf16[128,2048]{1,0:T(8,128)(2,1)} copy(bf16[128,2048]{1,0:T(8,128)(2,1)} %get-tuple-element.31) | data formatting | bytes 1048576
  167.0 1.8 %copy.20 = bf16[1,256,768]{2,1,0:T(8,128)(2,1)} copy(bf16[1,256,768]{2,1,0:T(8,128)(2,1)} %bitcast.58) | data formatting | bytes 786432
  168.7 0.7 copy.21
  169.5 0.7 copy.22
  (19 shorter events, 0.2 us)
Async XLA Ops:
  0.6 90.9 %copy-start = (bf16[1,2048,768]{2,1,0:T(8,128)(2,1)S(1)}, bf16[1,2048,768]{2,1,0:T(8,128)(2,1)}, u32[]{:S(2)}) copy-start(bf16[1,2048,768]{2,1,0:T(8,128)(2,1)} %param.12) | copy-start | bytes 9437188
  87.2 2.5 %copy-start.6 = (bf16[1,768,2048]{2,1,0:T(8,128)(2,1)S(1)}, bf16[1,768,2048]{2,1,0:T(8,128)(2,1)}, u32[]{:S(2)}) copy-start(bf16[1,768,2048]{2,1,0:T(8,128)(2,1)} %param.13) | copy-start | bytes 9437188
  89.7 1.9 %copy-start.7 = (bf16[4,128,2048]{2,1,0:T(8,128)(2,1)S(1)}, bf16[4,128,2048]{2,1,0:T(8,128)(2,1)}, u32[]{:S(2)}) copy-start(bf16[4,128,2048]{2,1,0:T(8,128)(2,1)} %get-tuple-element.15) | copy-start | bytes 6291460
  89.7 2.0 %copy-start.8 = (f32[512,768]{1,0:T(8,128)S(1)}, f32[512,768]{1,0:T(8,128)}, u32[]{:S(2)}) copy-start(f32[512,768]{1,0:T(8,128)} %fusion.5) | copy-start | bytes 4718596
  91.7 2.3 %copy-start.5 = (bf16[1,2048,768]{2,1,0:T(8,128)(2,1)S(1)}, bf16[1,2048,768]{2,1,0:T(8,128)(2,1)}, u32[]{:S(2)}) copy-start(bf16[1,2048,768]{2,1,0:T(8,128)(2,1)} %param.11) | copy-start | bytes 9437188
  95.9 3.2 %copy-start.1 = (bf16[4,128,2048]{2,1,0:T(8,128)(2,1)S(1)}, bf16[4,128,2048]{2,1,0:T(8,128)(2,1)}, u32[]{:S(2)}) copy-start(bf16[4,128,2048]{2,1,0:T(8,128)(2,1)} %get-tuple-element.14) | copy-start | bytes 6291460
  111.2 53.3 %copy-start.4 = (s32[128,2]{0,1:T(2,128)S(1)}, s32[128,2]{0,1:T(2,128)}, u32[]{:S(2)}) copy-start(s32[128,2]{0,1:T(2,128)} %param.9) | copy-start | bytes 3076
  163.1 6.3 %copy-start.2 = (bf16[96,2048]{1,0:T(8,128)(2,1)S(1)}, bf16[96,2048]{1,0:T(8,128)(2,1)}, u32[]{:S(2)}) copy-start(bf16[96,2048]{1,0:T(8,128)(2,1)} %get-tuple-element.20) | copy-start | bytes 1179652
  164.5 4.2 %copy-start.3 = (bf16[256,768]{1,0:T(8,128)(2,1)S(1)}, bf16[256,768]{1,0:T(8,128)(2,1)}, u32[]{:S(2)}) copy-start(bf16[256,768]{1,0:T(8,128)(2,1)} %get-tuple-element.19) | copy-start | bytes 1179652
